TPU v7x, 32 devices: a whole 2x2x4 slice. The times are simulated.
32 devices in a mesh: atoms: 8 (over z, y), modes: 4 (over x, core).
Axes of the slice: x: 2, y: 2, z: 4, core: 2. Of those that a mesh axis runs over, the one named last changes fastest.
Arguments:
- eigvec: bfloat16 [3072, 2048], P('atoms', 'modes'), may hold values from -6 to 6
- operator_blocks: bfloat16 [24, 8, 128, 128], P('atoms'), may hold values from -0.0034179688 to 0.0034179688
- column_blocks: int32 [24, 8], P('atoms'), may hold values from 0 to 23, as said below
- block_mask: int32 [24, 8], P('atoms'), may hold values 0 or 1
- spectrum: float32 [3072], replicated, may hold values from 0.5 to 20
- mode_index: int32 [2048], replicated, may hold values from 0 to 3071
- linewidth: float32 [2048], replicated, may hold values from 0.05 to 1
Outputs:
- flux_tiles: float32 [2048, 2048], P('modes', 'atoms')
- diffusivity: float32 [2048], P('modes')
Inputs may be any that keep to these rules, and one draw needn't show every extreme that they name: `column_blocks`: the 8 column blocks of row block r are distinct and lie within 4 blocks of r, counted around the cycle of 24 blocks.
All inputs are finite; a program needn't handle non-finite values. No bound on the sum of `block_mask` on one device may be relied on, other than what follows from the above.
Results may differ from a plain program's by a relative error of at most 0.0058.
Values may be sent and summed in bfloat16 or wider, within the bound.
No kernel may reach another device: no remote copies, remote signals or barrier semaphores. Data moves between devices by JAX's collectives and lax.ppermute only.
A program may use at most 64 MiB of HBM per device.

v0:
```python
import jax
import jax.numpy as jnp
from jax import lax
from jax.sharding import PartitionSpec as P

REACH = 4


def with_halo(block, sides, width):
    for axis, dim in sides:
        count = lax.axis_size(axis)
        forward = [(i, i + 1) for i in range(count - 1)]
        forward.append((count - 1, 0))
        backward = [(target, source) for source, target in forward]
        low = lax.ppermute(
            lax.slice_in_dim(block, block.shape[dim] - width, None, axis=dim), axis, forward
        )
        high = lax.ppermute(lax.slice_in_dim(block, 0, width, axis=dim), axis, backward)
        block = jnp.concatenate([low, block, high], axis=dim)
    return block


def from_behind(value, axis, by):
    devices = lax.axis_size(axis)
    return lax.ppermute(value, axis, [(i, (i + by) % devices) for i in range(devices)])


def pair_weight(row_freq, col_freq, row_width, col_width):
    freq_sum = row_freq[:, None] + col_freq[None, :]
    spacing = row_freq[:, None] - col_freq[None, :]
    mean_width = 0.5 * (row_width[:, None] + col_width[None, :])
    factor = freq_sum * freq_sum / (4.0 * row_freq[:, None] * col_freq[None, :])
    return factor * mean_width / (spacing * spacing + mean_width * mean_width)


def body(eigvec, operator_blocks, column_blocks, block_mask, spectrum, mode_index, linewidth):
    block_width = operator_blocks.shape[2]
    local_blocks = operator_blocks.shape[0]
    own_modes = eigvec.shape[1]
    atom_count = lax.axis_size("atoms")
    atom_rank = lax.axis_index("atoms")
    group_rank = lax.axis_index("modes")
    total_blocks = local_blocks * atom_count
    near_blocks = min(REACH, local_blocks)
    extra_blocks = REACH - near_blocks
    extended = with_halo(eigvec, (("atoms", 0),), near_blocks * block_width)
    far_pieces = []
    slab_rows = eigvec.shape[0]
    for distance, far_rows in (
        (2, eigvec[slab_rows - extra_blocks * block_width :]),
        (-2, eigvec[: extra_blocks * block_width]),
    ):
        far_pieces.append(from_behind(far_rows, "atoms", distance))
    extended = jnp.concatenate([far_pieces[0], extended, far_pieces[1]], axis=0)
    ext_blocks = extended.reshape(-1, block_width, own_modes)
    offsets = (column_blocks - atom_rank * local_blocks + REACH) % total_blocks
    picked = ext_blocks[offsets]
    masked = jnp.where(
        block_mask[:, :, None, None] > 0, operator_blocks, jnp.zeros((), operator_blocks.dtype)
    )
    product = jnp.einsum("bsij,bsjm->bim", masked, picked, preferred_element_type=jnp.float32)
    velocity = product.reshape(-1, own_modes).astype(jnp.bfloat16)
    contract = (((0,), (0,)), ((), ()))
    stacked = jnp.stack((eigvec, velocity))
    piece = lax.all_gather(stacked, "modes", axis=2, tiled=True)
    direct = lax.dot_general(eigvec, piece[1], contract, preferred_element_type=jnp.float32)
    mirror = lax.dot_general(velocity, piece[0], contract, preferred_element_type=jnp.float32)
    partial_flux = direct - mirror
    frequency = spectrum[mode_index]
    mode_total = frequency.shape[0]
    row_freq = lax.dynamic_slice_in_dim(frequency, group_rank * own_modes, own_modes)
    row_width = lax.dynamic_slice_in_dim(linewidth, group_rank * own_modes, own_modes)
    flux_tiles = lax.psum_scatter(partial_flux, "atoms", scatter_dimension=1, tiled=True)
    share_cols = flux_tiles.shape[1]
    col_freq = lax.dynamic_slice_in_dim(frequency, atom_rank * share_cols, share_cols)
    col_width = lax.dynamic_slice_in_dim(linewidth, atom_rank * share_cols, share_cols)
    weight = pair_weight(row_freq, col_freq, row_width, col_width)
    partial_sums = jnp.sum(weight * flux_tiles * flux_tiles, axis=1)
    diffusivity = lax.psum(partial_sums, "atoms") / mode_total
    return (flux_tiles, diffusivity)


def solution(mesh):
    return jax.shard_map(
        body,
        mesh=mesh,
        in_specs=(
            P("atoms", "modes"),
            P("atoms", None, None, None),
            P("atoms", None),
            P("atoms", None),
            P(),
            P(),
            P(),
        ),
        out_specs=(P("modes", "atoms"), P("modes")),
        check_vma=False,
    )
```

profile of v0, /device:TPU:0, one launch (start us, length us, event | category | flops | bytes accessed | tf_op | source)
XLA Modules:
  0.0 190.7 jit_solution(3013276178611091838)
XLA Ops:
  7.2 0.0 all-gather.2.cloned.1.call-start
  7.2 3.0 %collective-permute-start.1 = (bf16[384,512]{1,0:T(8,128)(2,1)}, bf16[384,512]{1,0:T(8,128)(2,1)S(1)}, u32[]{:S(2)}, u32[]{:S(2)}) collective-permute-start(bf16[384,512]{1,0:T(8,128)(2,1)} %param.7), channel_id=1, source_target_pairs={{0,4},{4,8},{8,12},{12,16},{16,20},{20,24},{24,28},{28,0},{1,5},{5... | collective-permute-start | bytes 1179656 | tf_op jit(solution)/shard_map/ppermute | solution.py:15
  10.3 3.1 %collective-permute-start.2 = (bf16[384,512]{1,0:T(8,128)(2,1)}, bf16[384,512]{1,0:T(8,128)(2,1)S(1)}, u32[]{:S(2)}, u32[]{:S(2)}) collective-permute-start(bf16[384,512]{1,0:T(8,128)(2,1)} %param.7), channel_id=1, source_target_pairs={{4,0},{8,4},{12,8},{16,12},{20,16},{24,20},{28,24},{0,28},{5,1},{9... | collective-permute-start | bytes 1179656 | tf_op jit(solution)/shard_map/ppermute | solution.py:18
  13.4 1.0 fusion.8
  14.4 0.1 collective-permute-start
  14.4 3.8 %collective-permute-start.3 = (bf16[128,512]{1,0:T(8,128)(2,1)S(1)}, bf16[128,512]{1,0:T(8,128)(2,1)S(1)}, u32[]{:S(2)}, u32[]{:S(2)}) collective-permute-start(bf16[128,512]{1,0:T(8,128)(2,1)S(1)} %get-tuple-element.8), channel_id=1, source_target_pairs={{0,24},{4,28},{8,0},{12,4},{16,8},{20,12},{24,16},{28,20},{1,25},{... | collective-permute-start | bytes 393224 | tf_op jit(solution)/shard_map/ppermute | solution.py:25
  18.3 0.7 compare_select_fusion.1
  19.0 1.2 broadcast_compare_fusion
  20.2 0.1 reshape.31
  20.2 8.0 %collective-permute-done = bf16[128,512]{1,0:T(8,128)(2,1)S(1)} collective-permute-done((bf16[128,512]{1,0:T(8,128)(2,1)S(1)}, bf16[128,512]{1,0:T(8,128)(2,1)S(1)}, u32[]{:S(2)}, u32[]{:S(2)}) %collective-permute-start) | collective-permute-done | bytes 131104 | tf_op jit(solution)/shard_map/ppermute | solution.py:25
  28.4 1.1 collective-permute-done.2
  29.6 1.1 copy-done.1
  30.7 2.1 %gather_fusion = bf16[24,128,512]{2,1,0:T(8,128)(2,1)S(1)} fusion(bf16[11,128,512]{2,1,0:T(8,128)(2,1)} %bitcast.22, s32[1024]{0:T(1024)S(1)} %pad_clamp_fusion), kind=kCustom, calls=%fused_computation | custom fusion | bytes 6291552 | tf_op jit(solution)/shard_map/gather | solution.py:57
  32.8 1.8 fusion.1
  34.6 0.7 copy-done.4
  35.3 1.0 pad_maximum_fusion
  36.3 0.0 all-gather.2.cloned.1.call-update
  36.3 0.0 reduce-scatter.2.cloned.1.call-start
  36.4 28.7 %all-gather.2.cloned.1.call-done = bf16[2,384,2048]{2,1,0:T(8,128)(2,1)} async-done(((bf16[2,384,512]{2,1,0:T(8,128)(2,1)}), bf16[2,384,2048]{2,1,0:T(8,128)(2,1)}) %all-gather.2.cloned.1.call-update) | async-done | bytes 3145744 | tf_op jit(solution)/shard_map/all_gather | solution.py:65
  65.1 2.9 %fusion = f32[2048,512]{1,0:T(8,128)S(1)} fusion(bf16[384,512]{1,0:T(8,128)(2,1)S(1)} %copy-done.2, bf16[2,384,2048]{2,1,0:T(8,128)(2,1)} %all-gather.2.cloned.1.call-done), kind=kOutput, calls=%fused_computation.5 | convolution fusion | flops 805306368 | bytes 6160384 | tf_op jit(solution)/shard_map/dot_general | solution.py:66
  68.0 3.3 %bitcast_subtract_fusion = f32[512,2048]{0,1:T(8,128)} fusion(f32[2048,512]{1,0:T(8,128)S(1)} %fusion, bf16[384,512]{1,0:T(8,128)(2,1)S(1)} %bitcast.25, bf16[2,384,2048]{2,1,0:T(8,128)(2,1)S(1)} %copy-done.3), kind=kOutput, calls=%fused_computation.2 | convolution fusion | flops 806354944 | bytes 10354688 | tf_op jit(solution)/shard_map/dot_general | solution.py:67
  71.3 0.7 copy-done.6
  71.9 11.8 %gather_fusion.1 = f32[2048]{0:T(1024)S(1)} fusion(f32[3072]{0:T(1024)S(1)} %copy-done, s32[2048]{0:T(1024)S(1)} %fusion.6), kind=kCustom, calls=%fused_computation.1 | custom fusion | bytes 24576 | tf_op jit(solution)/shard_map/gather | solution.py:69
  83.7 0.1 dynamic_slice.13
  83.8 0.8 dynamic_slice.15
  84.6 0.8 dynamic_slice.14
  85.3 0.1 broadcast_multiply_fusion.1
  85.4 74.3 %reduce-scatter.2.cloned.1.call-done = f32[512,256]{0,1:T(8,128)} async-done(((f32[512,2048]{0,1:T(8,128)}), f32[512,256]{0,1:T(8,128)}) %reduce-scatter.2.cloned.1.call-update) | async-done | bytes 524304 | tf_op jit(solution)/shard_map/reduce_scatter | solution.py:73
  159.7 1.4 fusion.4
  161.2 20.1 %psum.7 = f32[512]{0:T(512)S(1)} all-reduce(f32[512]{0:T(512)S(1)} %fusion.4), channel_id=1, replica_groups=mesh['atoms'=8,'modes'=4] {'atoms'}, use_global_device_ids=true, to_apply=%region_2.3 | all-reduce | flops 512 | bytes 4096 | tf_op jit(solution)/shard_map/psum | solution.py:79
  181.2 0.6 broadcast_multiply_fusion
  181.8 2.0 %copy.12 = f32[512,256]{1,0:T(8,128)} copy(f32[512,256]{0,1:T(8,128)} %reduce-scatter.2.cloned.1.call-done) | data formatting | bytes 1048576
  (21 shorter events, 0.2 us)
Async XLA Ops:
  7.2 64.8 %copy-start = (f32[3072]{0:T(1024)S(1)}, f32[3072]{0:T(1024)}, u32[]{:S(2)}) copy-start(f32[3072]{0:T(1024)} %param.11) | copy-start | bytes 36868
  7.2 21.2 %copy-start.2 = (bf16[384,512]{1,0:T(8,128)(2,1)S(1)}, bf16[384,512]{1,0:T(8,128)(2,1)}, u32[]{:S(2)}) copy-start(bf16[384,512]{1,0:T(8,128)(2,1)} %param.7) | copy-start | bytes 1179652
  7.2 57.9 %all-gather.2.cloned.1.call-start = ((), (), s32[]{:S(2)}) async-start(), calls=%async_computation.1 | async-start | bytes 3932160 | tf_op jit(solution)/shard_map/all_gather | solution.py:65
  7.2 21.1 %collective-permute-start.1 = (bf16[384,512]{1,0:T(8,128)(2,1)}, bf16[384,512]{1,0:T(8,128)(2,1)S(1)}, u32[]{:S(2)}, u32[]{:S(2)}) collective-permute-start(bf16[384,512]{1,0:T(8,128)(2,1)} %param.7), channel_id=1, source_target_pairs={{0,4},{4,8},{8,12},{12,16},{16,20},{20,24},{24,28},{28,0},{1,5},{5... | collective-permute-start | bytes 1179656 | tf_op jit(solution)/shard_map/ppermute | solution.py:15
  10.3 19.2 %collective-permute-start.2 = (bf16[384,512]{1,0:T(8,128)(2,1)}, bf16[384,512]{1,0:T(8,128)(2,1)S(1)}, u32[]{:S(2)}, u32[]{:S(2)}) collective-permute-start(bf16[384,512]{1,0:T(8,128)(2,1)} %param.7), channel_id=1, source_target_pairs={{4,0},{8,4},{12,8},{16,12},{20,16},{24,20},{28,24},{0,28},{5,1},{9... | collective-permute-start | bytes 1179656 | tf_op jit(solution)/shard_map/ppermute | solution.py:18
  14.4 13.9 %collective-permute-start = (bf16[128,512]{1,0:T(8,128)(2,1)S(1)}, bf16[128,512]{1,0:T(8,128)(2,1)S(1)}, u32[]{:S(2)}, u32[]{:S(2)}) collective-permute-start(bf16[128,512]{1,0:T(8,128)(2,1)S(1)} %get-tuple-element.9), channel_id=1, source_target_pairs={{0,8},{4,12},{8,16},{12,20},{16,24},{20,28},{24,0},{28,4},{1,9},{5... | collective-permute-start | bytes 393224 | tf_op jit(solution)/shard_map/ppermute | solution.py:25
  14.4 15.1 %collective-permute-start.3 = (bf16[128,512]{1,0:T(8,128)(2,1)S(1)}, bf16[128,512]{1,0:T(8,128)(2,1)S(1)}, u32[]{:S(2)}, u32[]{:S(2)}) collective-permute-start(bf16[128,512]{1,0:T(8,128)(2,1)S(1)} %get-tuple-element.8), channel_id=1, source_target_pairs={{0,24},{4,28},{8,0},{12,4},{16,8},{20,12},{24,16},{28,20},{1,25},{... | collective-permute-start | bytes 393224 | tf_op jit(solution)/shard_map/ppermute | solution.py:25
  29.6 1.1 copy-start.1
  34.6 0.7 copy-start.4
  36.3 31.6 %copy-start.5 = (bf16[3,128,512]{2,1,0:T(8,128)(2,1)S(1)}, bf16[3,128,512]{2,1,0:T(8,128)(2,1)}, u32[]{:S(2)}) copy-start(bf16[3,128,512]{2,1,0:T(8,128)(2,1)} %copy-done.4) | copy-start | bytes 1179652
  36.3 123.4 %reduce-scatter.2.cloned.1.call-start = ((), (), s32[]{:S(2)}) async-start(), calls=%async_computation.2 | async-start | bytes 4718592 | tf_op jit(solution)/shard_map/reduce_scatter | solution.py:73
  65.1 2.9 %copy-start.3 = (bf16[2,384,2048]{2,1,0:T(8,128)(2,1)S(1)}, bf16[2,384,2048]{2,1,0:T(8,128)(2,1)}, u32[]{:S(2)}) copy-start(bf16[2,384,2048]{2,1,0:T(8,128)(2,1)} %all-gather.2.cloned.1.call-done) | copy-start | bytes 9437188
  71.2 0.7 copy-start.6
Sparse Core Ops, SparseCore 0:
  36.4 28.6 all-gather.1
  71.4 88.2 reduce-scatter.1
where the time goes:
time: 191 us
  waiting for transfers between devices  112 us (59%)
  local copies, waits for them, and re-layouts  21.3 us (11%)
  blocking collectives  20.1 us (11%)
  between operations  14.2 us (7%)
  starting transfers between devices  10.1 us (5%)
  matrix products  7.9 us (4%)
  other arithmetic  4.96 us (3%)
    reduce_scatter x1, waiting for transfers between devices, body(): lax.psum_scatter(partial_flux, 'atoms', scatter_dimension=1, tiled=True)  74.3 us
    all_gather x1, waiting for transfers between devices, body(): piece = lax.all_gather(stacked, 'modes', axis=2, tiled=True)  28.7 us
    psum x1, blocking collectives, body(): diffusivity = lax.psum(partial_sums, 'atoms') / mode_total  20.1 us
    gather x1, local copies, waits for them, and re-layouts, body(): frequency = spectrum[mode_index]  11.8 us
    ppermute x2, waiting for transfers between devices, from_behind(): lax.ppermute(value, axis, [(i, (i + by) % devices) for i in range(devices)])  8.03 us
    unnamed x19, local copies, waits for them, and re-layouts  4.68 us
    ppermute x2, starting transfers between devices, from_behind(): lax.ppermute(value, axis, [(i, (i + by) % devices) for i in range(devices)])  3.87 us
  transfers between devices with their start and end apart: 6, of which 4 were waited for; matrix products, arithmetic and copies ran while one was open for 9% of the time, Pallas kernels for 0%

commit v1 on v0

--- a/solution.py
+++ b/solution.py
@@ -62,7 +62,8 @@
     velocity = product.reshape(-1, own_modes).astype(jnp.bfloat16)
     contract = (((0,), (0,)), ((), ()))
     stacked = jnp.stack((eigvec, velocity))
-    piece = lax.all_gather(stacked, "modes", axis=2, tiled=True)
+    parts = lax.all_gather(stacked, "modes", axis=0, tiled=False)
+    piece = jnp.concatenate(parts, axis=2)
     direct = lax.dot_general(eigvec, piece[1], contract, preferred_element_type=jnp.float32)
     mirror = lax.dot_general(velocity, piece[0], contract, preferred_element_type=jnp.float32)
     partial_flux = direct - mirror

time: 191 us -> 200 us (1.047)
  local copies, waits for them, and re-layouts: 21.3 us -> 27.5 us
  matrix products: 7.9 us -> 10.3 us
    slice x0 -> x3, local copies, waits for them, and re-layouts: none -> 6.09 us  [the longest x2 4.2 us: body(): piece[0]]
    dot_general x1, matrix products: 3.27 us -> 5.38 us  [body(): lax.dot_general(velocity, piece[0], contract, preferred_element_type=jnp....]
    unnamed x19 -> x17, local copies, waits for them, and re-layouts: 4.68 us -> 4.8 us
  transfers between devices with their start and end apart: 6 -> 6, of which waited for: 4 -> 4; matrix products, arithmetic and copies ran while one was open for 9% -> 8% of each run, Pallas kernels for 0% -> 0%
where the time goes in v1:
time: 200 us; the launch traced here: 199 us
  waiting for transfers between devices  112 us (56%)
  local copies, waits for them, and re-layouts  27.5 us (14%)
  blocking collectives  20.1 us (10%)
  between operations  14.2 us (7%)
  matrix products  10.3 us (5%)
  starting transfers between devices  10.1 us (5%)
  other arithmetic  4.96 us (2%)
    reduce_scatter x1, waiting for transfers between devices, body(): lax.psum_scatter(partial_flux, 'atoms', scatter_dimension=1, tiled=True)  74.3 us
    all_gather x1, waiting for transfers between devices, body(): parts = lax.all_gather(stacked, 'modes', axis=0, tiled=False)  28.7 us
    psum x1, blocking collectives, body(): diffusivity = lax.psum(partial_sums, 'atoms') / mode_total  20.1 us
    gather x1, local copies, waits for them, and re-layouts, body(): frequency = spectrum[mode_index]  11.8 us
    ppermute x2, waiting for transfers between devices, from_behind(): lax.ppermute(value, axis, [(i, (i + by) % devices) for i in range(devices)])  8.03 us
    dot_general x1, matrix products, body(): lax.dot_general(velocity, piece[0], contract, preferred_element_type=jnp....  5.38 us
    unnamed x17, local copies, waits for them, and re-layouts  4.8 us
    slice x2, local copies, waits for them, and re-layouts, body(): piece[0]  4.2 us
  transfers between devices with their start and end apart: 6, of which 4 were waited for; matrix products, arithmetic and copies ran while one was open for 8% of the time, Pallas kernels for 0%

profile of v1, /device:TPU:0, one launch (start us, length us, event | category | flops | bytes accessed | tf_op | source)
XLA Modules:
  0.0 199.3 jit_solution(713083046490102267)
XLA Ops:
  7.2 3.0 %collective-permute-start.1 = (bf16[384,512]{1,0:T(8,128)(2,1)}, bf16[384,512]{1,0:T(8,128)(2,1)S(1)}, u32[]{:S(2)}, u32[]{:S(2)}) collective-permute-start(bf16[384,512]{1,0:T(8,128)(2,1)} %param.7), channel_id=1, source_target_pairs={{0,4},{4,8},{8,12},{12,16},{16,20},{20,24},{24,28},{28,0},{1,5},{5... | collective-permute-start | bytes 1179656 | tf_op jit(solution)/shard_map/ppermute | solution.py:15
  10.3 3.1 %collective-permute-start.2 = (bf16[384,512]{1,0:T(8,128)(2,1)}, bf16[384,512]{1,0:T(8,128)(2,1)S(1)}, u32[]{:S(2)}, u32[]{:S(2)}) collective-permute-start(bf16[384,512]{1,0:T(8,128)(2,1)} %param.7), channel_id=1, source_target_pairs={{4,0},{8,4},{12,8},{16,12},{20,16},{24,20},{28,24},{0,28},{5,1},{9... | collective-permute-start | bytes 1179656 | tf_op jit(solution)/shard_map/ppermute | solution.py:18
  13.4 1.0 fusion.8
  14.4 3.8 %collective-permute-start.3 = (bf16[128,512]{1,0:T(8,128)(2,1)S(1)}, bf16[128,512]{1,0:T(8,128)(2,1)S(1)}, u32[]{:S(2)}, u32[]{:S(2)}) collective-permute-start(bf16[128,512]{1,0:T(8,128)(2,1)S(1)} %get-tuple-element.14), channel_id=1, source_target_pairs={{0,24},{4,28},{8,0},{12,4},{16,8},{20,12},{24,16},{28,20},{1,25},{... | collective-permute-start | bytes 393224 | tf_op jit(solution)/shard_map/ppermute | solution.py:25
  18.3 0.7 compare_select_fusion.1
  19.0 1.2 broadcast_compare_fusion
  20.2 0.1 reshape.40
  20.2 8.0 %collective-permute-done = bf16[128,512]{1,0:T(8,128)(2,1)S(1)} collective-permute-done((bf16[128,512]{1,0:T(8,128)(2,1)S(1)}, bf16[128,512]{1,0:T(8,128)(2,1)S(1)}, u32[]{:S(2)}, u32[]{:S(2)}) %collective-permute-start) | collective-permute-done | bytes 131104 | tf_op jit(solution)/shard_map/ppermute | solution.py:25
  28.4 1.1 collective-permute-done.2
  29.6 1.1 copy-done.1
  30.7 2.1 %gather_fusion = bf16[24,128,512]{2,1,0:T(8,128)(2,1)S(1)} fusion(bf16[11,128,512]{2,1,0:T(8,128)(2,1)} %bitcast.24, s32[1024]{0:T(1024)S(1)} %pad_clamp_fusion), kind=kCustom, calls=%fused_computation | custom fusion | bytes 6291552 | tf_op jit(solution)/shard_map/gather | solution.py:57
  32.8 1.8 fusion
  34.6 0.7 copy-done.3
  35.3 1.0 pad_maximum_fusion
  36.4 28.7 %all-gather.3.cloned.1.call-done = bf16[8,384,512]{2,1,0:T(8,128)(2,1)} async-done(((bf16[2,384,512]{2,1,0:T(8,128)(2,1)}), bf16[8,384,512]{2,1,0:T(8,128)(2,1)}) %all-gather.3.cloned.1.call-update) | async-done | bytes 3145744 | tf_op jit(solution)/shard_map/all_gather | solution.py:65
  65.1 3.3 %fusion.7 = (bf16[1,384,4,512]{3,1,0,2:T(8,128)(2,1)S(1)}, bf16[1,384,4,512]{3,1,0,2:T(8,128)(2,1)}) fusion(bf16[2,384,4,512]{3,1,0,2:T(8,128)(2,1)} %bitcast.29), kind=kLoop, calls=%fused_computation.26 | loop fusion | bytes 6291456 | tf_op jit(solution)/shard_map/slice | solution.py:68
  68.4 1.9 copy.17
  70.3 3.2 %fusion.9 = f32[2048,512]{1,0:T(8,128)} fusion(bf16[384,2048]{0,1:T(8,128)(2,1)S(1)} %bitcast.23, bf16[384,512]{1,0:T(8,128)(2,1)S(1)} %copy-done.2), kind=kOutput, calls=%fused_computation.28 | convolution fusion | flops 805306368 | bytes 6160384 | tf_op jit(solution)/shard_map/dot_general | solution.py:67
  73.5 0.9 copy.18
  74.4 0.1 copy-done.4
  74.5 5.4 %bitcast_subtract_fusion = f32[512,2048]{0,1:T(8,128)} fusion(f32[2048,512]{1,0:T(8,128)} %fusion.9, bf16[384,2048]{0,1:T(8,128)(2,1)S(1)} %bitcast.25, bf16[384,512]{1,0:T(8,128)(2,1)S(1)} %bitcast.28), kind=kOutput, calls=%fused_computation.2 | convolution fusion | flops 806354944 | bytes 10354688 | tf_op jit(solution)/shard_map/dot_general | solution.py:68
  79.9 0.7 copy-done.5
  80.6 11.8 %gather_fusion.1 = f32[2048]{0:T(1024)S(1)} fusion(f32[3072]{0:T(1024)S(1)} %copy-done, s32[2048]{0:T(1024)S(1)} %fusion.5), kind=kCustom, calls=%fused_computation.1 | custom fusion | bytes 24576 | tf_op jit(solution)/shard_map/gather | solution.py:70
  92.4 0.1 dynamic_slice.13
  92.5 0.8 dynamic_slice.15
  93.2 0.8 dynamic_slice.14
  94.0 0.1 broadcast_multiply_fusion.1
  94.1 74.3 %reduce-scatter.2.cloned.1.call-done = f32[512,256]{0,1:T(8,128)} async-done(((f32[512,2048]{0,1:T(8,128)}), f32[512,256]{0,1:T(8,128)}) %reduce-scatter.2.cloned.1.call-update) | async-done | bytes 524304 | tf_op jit(solution)/shard_map/reduce_scatter | solution.py:74
  168.4 1.4 fusion.3
  169.8 20.1 %psum.7 = f32[512]{0:T(512)S(1)} all-reduce(f32[512]{0:T(512)S(1)} %fusion.3), channel_id=1, replica_groups=mesh['atoms'=8,'modes'=4] {'atoms'}, use_global_device_ids=true, to_apply=%region_2.3 | all-reduce | flops 512 | bytes 4096 | tf_op jit(solution)/shard_map/psum | solution.py:80
  189.9 0.6 broadcast_multiply_fusion
  190.5 2.0 %copy.20 = f32[512,256]{1,0:T(8,128)} copy(f32[512,256]{0,1:T(8,128)} %reduce-scatter.2.cloned.1.call-done) | data formatting | bytes 1048576
  (22 shorter events, 0.3 us)
Async XLA Ops:
  7.2 73.4 %copy-start = (f32[3072]{0:T(1024)S(1)}, f32[3072]{0:T(1024)}, u32[]{:S(2)}) copy-start(f32[3072]{0:T(1024)} %param.11) | copy-start | bytes 36868
  7.2 21.2 %copy-start.2 = (bf16[384,512]{1,0:T(8,128)(2,1)S(1)}, bf16[384,512]{1,0:T(8,128)(2,1)}, u32[]{:S(2)}) copy-start(bf16[384,512]{1,0:T(8,128)(2,1)} %param.7) | copy-start | bytes 1179652
  7.2 57.9 %all-gather.3.cloned.1.call-start = ((), (), s32[]{:S(2)}) async-start(), calls=%async_computation.2 | async-start | bytes 3932160 | tf_op jit(solution)/shard_map/all_gather | solution.py:65
  7.2 21.1 %collective-permute-start.1 = (bf16[384,512]{1,0:T(8,128)(2,1)}, bf16[384,512]{1,0:T(8,128)(2,1)S(1)}, u32[]{:S(2)}, u32[]{:S(2)}) collective-permute-start(bf16[384,512]{1,0:T(8,128)(2,1)} %param.7), channel_id=1, source_target_pairs={{0,4},{4,8},{8,12},{12,16},{16,20},{20,24},{24,28},{28,0},{1,5},{5... | collective-permute-start | bytes 1179656 | tf_op jit(solution)/shard_map/ppermute | solution.py:15
  10.3 19.2 %collective-permute-start.2 = (bf16[384,512]{1,0:T(8,128)(2,1)}, bf16[384,512]{1,0:T(8,128)(2,1)S(1)}, u32[]{:S(2)}, u32[]{:S(2)}) collective-permute-start(bf16[384,512]{1,0:T(8,128)(2,1)} %param.7), channel_id=1, source_target_pairs={{4,0},{8,4},{12,8},{16,12},{20,16},{24,20},{28,24},{0,28},{5,1},{9... | collective-permute-start | bytes 1179656 | tf_op jit(solution)/shard_map/ppermute | solution.py:18
  14.4 13.9 %collective-permute-start = (bf16[128,512]{1,0:T(8,128)(2,1)S(1)}, bf16[128,512]{1,0:T(8,128)(2,1)S(1)}, u32[]{:S(2)}, u32[]{:S(2)}) collective-permute-start(bf16[128,512]{1,0:T(8,128)(2,1)S(1)} %get-tuple-element.15), channel_id=1, source_target_pairs={{0,8},{4,12},{8,16},{12,20},{16,24},{20,28},{24,0},{28,4},{1,9},{5... | collective-permute-start | bytes 393224 | tf_op jit(solution)/shard_map/ppermute | solution.py:25
  14.4 15.1 %collective-permute-start.3 = (bf16[128,512]{1,0:T(8,128)(2,1)S(1)}, bf16[128,512]{1,0:T(8,128)(2,1)S(1)}, u32[]{:S(2)}, u32[]{:S(2)}) collective-permute-start(bf16[128,512]{1,0:T(8,128)(2,1)S(1)} %get-tuple-element.14), channel_id=1, source_target_pairs={{0,24},{4,28},{8,0},{12,4},{16,8},{20,12},{24,16},{28,20},{1,25},{... | collective-permute-start | bytes 393224 | tf_op jit(solution)/shard_map/ppermute | solution.py:25
  29.6 1.1 copy-start.1
  34.6 0.7 copy-start.3
  36.3 132.0 %reduce-scatter.2.cloned.1.call-start = ((), (), s32[]{:S(2)}) async-start(), calls=%async_computation.1 | async-start | bytes 4718592 | tf_op jit(solution)/shard_map/reduce_scatter | solution.py:74
  73.5 1.0 copy-start.4
  79.9 0.7 copy-start.5
Sparse Core Ops, SparseCore 0:
  36.4 28.6 all-gather.2
  80.0 88.2 reduce-scatter.1
